TPU v7x, 32 devices: a whole 2x2x4 slice. The times are simulated.
32 devices in a mesh: seq: 8 (over z, x), res: 4 (over y, core).
Axes of the slice: x: 2, y: 2, z: 4, core: 2. Of those that a mesh axis runs over, the one named last changes fastest.
Arguments:
- alignment: bfloat16 [128, 256, 256], P('res', 'seq'), may hold values from -6 to 6
- alignment_mask: int32 [128, 256], P('res', 'seq'), may hold values from 0 to 1, as said below
- residue_mask: int32 [256], replicated, may hold values from 0 to 1, as said below
- pair_input: float32 [256, 256, 128], P('seq', 'res'), may hold values from -6 to 6
- outer_gain: float32 [256], replicated, may hold values from 0.25 to 1.75
- left_weight: bfloat16 [256, 32], replicated, may hold values from -0.375 to 0.375
- right_weight: bfloat16 [256, 32], replicated, may hold values from -0.375 to 0.375
- outer_weight: bfloat16 [1024, 128], replicated, may hold values from -1 to 1
- pair_gain: float32 [128], replicated, may hold values from 0.25 to 1.75
- bias_weight: bfloat16 [128, 8], replicated, may hold values from -48 to 48
- row_gain: float32 [256], replicated, may hold values from 0.25 to 1.75
- query_weight: bfloat16 [256, 256], replicated, may hold values from -0.375 to 0.375
- key_weight: bfloat16 [256, 256], replicated, may hold values from -0.375 to 0.375
- value_weight: bfloat16 [256, 256], replicated, may hold values from -0.375 to 0.375
- gate_weight: bfloat16 [256, 256], replicated, may hold values from -0.375 to 0.375
- output_weight: bfloat16 [256, 256], replicated, may hold values from -2 to 2
- transition_gain: float32 [256], replicated, may hold values from 0.25 to 1.75
- up_weight: bfloat16 [256, 1024], replicated, may hold values from -0.375 to 0.375
- down_weight: bfloat16 [1024, 256], replicated, may hold values from -0.1875 to 0.1875
Outputs:
- pair_output: float32 [256, 256, 128], P('seq', 'res')
- alignment_output: float32 [128, 256, 256], P('res', 'seq')
Inputs may be any that keep to these rules, and one draw needn't show every extreme that they name: `residue_mask`: 1 for a present residue, 0 for padding; at least one residue is 1 and at least one is 0. Some residue whose residue_mask is 1 has alignment_mask 1 in every sequence.
All inputs are finite; a program needn't handle non-finite values.
Results may differ from a plain program's by a relative error of at most 0.04.
Values may be sent and summed in bfloat16 or wider, within the bound.
No kernel may reach another device: no remote copies, remote signals or barrier semaphores. Data moves between devices by JAX's collectives and lax.ppermute only.
A program may use at most 128 MiB of HBM per device.

v0:
```python
import math
import jax
import jax.numpy as jnp
from jax import lax
from jax.sharding import PartitionSpec as P

EPSILON = 1e-05
MASKED = -1000000000.0
SCORE_LIMIT = 524288


def layer_norm(values, scales):
    values = values.astype(jnp.float32)
    center = values - jnp.mean(values, -1, keepdims=True)
    spread = jnp.mean(center * center, -1, keepdims=True)
    return center * lax.rsqrt(spread + EPSILON) * scales


def project(values, weight):
    flattened = values.reshape(-1, values.shape[-1])
    result = jnp.dot(flattened, weight, preferred_element_type=jnp.float32)
    return result.reshape(values.shape[:-1] + (weight.shape[1],))


def block_size(length, per_item):
    item_limit = max(1, SCORE_LIMIT // per_item)
    return max(
        (
            divisor
            for divisor in range(1, length + 1)
            if length % divisor == 0 and divisor <= item_limit
        )
    )


def in_blocks(function, arrays, block_rows):
    shaped = tuple(
        (
            member.reshape((member.shape[0] // block_rows, block_rows) + member.shape[1:])
            for member in arrays
        )
    )
    outputs = lax.map(function, shaped)
    return jax.tree.map(lambda member: member.reshape((-1,) + member.shape[2:]), outputs)


def head_scores(query_rows, key_rows, live_keys, head_bias, head_count, score_scale):
    seq_block, row_count, features = query_rows.shape
    key_count = key_rows.shape[1]
    head_size = features // head_count
    scores = jnp.einsum(
        "sihd,sjhd->shij",
        query_rows.reshape(seq_block, row_count, head_count, head_size),
        key_rows.reshape(seq_block, key_count, head_count, head_size),
        preferred_element_type=jnp.float32,
    )
    scores = scores * score_scale + head_bias.astype(jnp.float32)[None]
    return jnp.where(live_keys[:, None, None, :] > 0, scores, MASKED)


def head_weigh(scores, score_peaks, values, head_count):
    weights = jnp.exp(scores - score_peaks[..., None])
    totals = jnp.swapaxes(jnp.sum(weights, -1), 1, 2)
    seq_block, key_count, features = values.shape
    mixed_sum = jnp.einsum(
        "shij,sjhd->sihd",
        weights.astype(jnp.bfloat16),
        values.reshape(seq_block, key_count, head_count, features // head_count),
        preferred_element_type=jnp.float32,
    )
    return (mixed_sum.reshape(seq_block, mixed_sum.shape[1], features), totals)


def on_device(
    alignment,
    alignment_mask,
    residue_mask,
    pair_input,
    outer_gain,
    left_weight,
    right_weight,
    outer_weight,
    pair_gain,
    bias_weight,
    row_gain,
    query_weight,
    key_weight,
    value_weight,
    gate_weight,
    output_weight,
    transition_gain,
    up_weight,
    down_weight,
):
    seq_share, row_count = (alignment.shape[0], alignment.shape[1])
    res_local = pair_input.shape[1]
    seq_total = seq_share * lax.axis_size("res")
    res_total = row_count * lax.axis_size("seq")
    head_count = bias_weight.shape[1]
    outer_width = left_weight.shape[1]
    pair_width = pair_input.shape[2]
    score_scale = (query_weight.shape[1] // head_count) ** (-0.5)
    residue_live = residue_mask.astype(jnp.float32)
    row_live = lax.dynamic_slice_in_dim(residue_live, lax.axis_index("seq") * row_count, row_count)
    column_live = lax.dynamic_slice_in_dim(
        residue_live, lax.axis_index("res") * res_local, res_local
    )
    mask_local = alignment_mask.astype(jnp.bfloat16)
    own_live = alignment_mask.astype(jnp.float32) * row_live[None, :]
    outer_norm = layer_norm(alignment, outer_gain).astype(jnp.bfloat16)
    row_norm = layer_norm(alignment, row_gain).astype(jnp.bfloat16)
    left_local = (project(outer_norm, left_weight) * own_live[..., None]).astype(jnp.bfloat16)
    left_proj, row_mask = (
        lax.all_gather(left_local, "res", axis=0, tiled=True),
        lax.all_gather(mask_local, "res", axis=0, tiled=True),
    )
    row_flags = (row_mask.astype(jnp.float32) * row_live[None, :]).astype(jnp.bfloat16)
    wide_alignment, wide_mask = (
        lax.all_gather(alignment, "seq", axis=1, tiled=True),
        lax.all_gather(mask_local, "seq", axis=1, tiled=True),
    )
    wide_live = wide_mask.astype(jnp.float32) * residue_live[None, :]
    key_norm = layer_norm(wide_alignment, row_gain).astype(jnp.bfloat16)
    outer_wide = layer_norm(wide_alignment, outer_gain).astype(jnp.bfloat16)
    all_keys = project(key_norm, key_weight).astype(jnp.bfloat16)
    all_values = project(key_norm, value_weight).astype(jnp.bfloat16)
    wide_right = (project(outer_wide, right_weight) * wide_live[..., None]).astype(jnp.bfloat16)
    right_proj, column_mask = (
        lax.all_to_all(wide_right, "res", split_axis=1, concat_axis=0, tiled=True),
        lax.all_to_all(wide_mask, "res", split_axis=1, concat_axis=0, tiled=True),
    )
    column_flags = (column_mask.astype(jnp.float32) * column_live[None, :]).astype(jnp.bfloat16)
    right_flat = right_proj.reshape(seq_total, res_local * outer_width)
    row_step = math.gcd(row_count, 16)

    def outer_rows(row_start):
        left_piece = lax.dynamic_slice_in_dim(left_proj, row_start, row_step, 1).reshape(
            seq_total, row_step * outer_width
        )
        product = lax.dot_general(
            left_piece, right_flat, (((0,), (0,)), ((), ())), preferred_element_type=jnp.float32
        )
        product = product.reshape(row_step, outer_width, res_local, outer_width).transpose(
            0, 2, 1, 3
        )
        product = product.reshape(row_step * res_local, outer_width * outer_width).astype(
            jnp.bfloat16
        )
        update = jnp.dot(product, outer_weight, preferred_element_type=jnp.float32).reshape(
            row_step, res_local, pair_width
        )
        live_rows = lax.dynamic_slice_in_dim(row_flags, row_start, row_step, 1)
        counts = lax.dot_general(
            live_rows, column_flags, (((0,), (0,)), ((), ())), preferred_element_type=jnp.float32
        )
        return update / jnp.maximum(counts, 1.0)[..., None]

    starts = jnp.arange(row_count // row_step, dtype=jnp.int32) * row_step
    outer_update = lax.map(outer_rows, starts).reshape(row_count, res_local, pair_width)
    pair_output = pair_input + outer_update
    pair_norm = layer_norm(pair_output, pair_gain).astype(jnp.bfloat16)
    pair_bias = jnp.einsum(
        "ijc,ch->hij", pair_norm, bias_weight, preferred_element_type=jnp.float32
    ).astype(jnp.bfloat16)
    full_bias = lax.all_gather(pair_bias, "res", axis=2, tiled=True)
    own_queries = project(row_norm, query_weight).astype(jnp.bfloat16)
    gate_values = jax.nn.sigmoid(project(row_norm, gate_weight))
    seq_step = block_size(seq_share, head_count * row_count * res_total)

    def attend_piece(members):
        query_piece, key_piece, value_piece, live_piece = members
        scores = head_scores(query_piece, key_piece, live_piece, full_bias, head_count, score_scale)
        return head_weigh(scores, jnp.max(scores, -1), value_piece, head_count)

    mixed_sum, totals = in_blocks(
        attend_piece, (own_queries, all_keys, all_values, wide_live), seq_step
    )
    attended = (
        mixed_sum.reshape(seq_share, row_count, head_count, -1) / totals[..., None]
    ).reshape(seq_share, row_count, -1)
    gated_rows = (attended * gate_values).astype(jnp.bfloat16)
    after_rows = alignment.astype(jnp.float32) + project(gated_rows, output_weight)
    trans_norm = layer_norm(after_rows, transition_gain).astype(jnp.bfloat16)
    hidden_units = jnp.maximum(project(trans_norm, up_weight), 0.0).astype(jnp.bfloat16)
    alignment_output = after_rows + project(hidden_units, down_weight)
    return (pair_output, alignment_output)


def solution(mesh):
    in_specs = (
        P("res", "seq", None),
        P("res", "seq"),
        P(),
        P("seq", "res", None),
        P(),
        P(),
        P(),
        P(),
        P(),
        P(),
        P(),
        P(),
        P(),
        P(),
        P(),
        P(),
        P(),
        P(),
        P(),
    )
    out_specs = (P("seq", "res", None), P("res", "seq", None))
    return jax.shard_map(
        on_device, mesh=mesh, in_specs=in_specs, out_specs=out_specs, check_vma=False
    )
```

profile of v0, /device:TPU:0, one launch (start us, length us, event | category | flops | bytes accessed | tf_op | source)
XLA Modules:
  0.0 229.8 jit_solution(551415257638649572)
XLA Ops:
  8.7 32.9 %all_gather.17 = bf16[32,256]{0,1:T(8,128)(2,1)S(1)} all-gather(bf16[32,32]{0,1:T(8,128)(2,1)S(1)} %convert_element_type.111), channel_id=1, replica_groups=mesh['seq'=8,'res'=4] {'seq'}, dimensions={1}, use_global_device_ids=true | all-gather | bytes 18432 | tf_op jit(solution)/shard_map/all_gather | solution.py:120
  42.4 3.3 %all-to-all-start.1 = ((bf16[4,2,1024]{2,1,0:T(2,128)(2,1)}), bf16[4,2,1024]{2,1,0:T(2,128)(2,1)S(1)}, u32[]{:S(2)}, u32[]{:S(2)}) async-start(bf16[4,2,1024]{2,1,0:T(2,128)(2,1)} %reshape.187), calls=%async_computation.1 | async-start | bytes 32768 | tf_op jit(solution)/shard_map/all_to_all | solution.py:130
  46.6 5.2 %all_gather.18 = bf16[128,32]{1,0:T(8,128)(2,1)S(1)} all-gather(bf16[32,32]{1,0:T(8,128)(2,1)S(1)} %copy.88), channel_id=1, replica_groups=mesh['seq'=8,'res'=4] {'res'}, dimensions={0}, use_global_device_ids=true | all-gather | bytes 10240 | tf_op jit(solution)/shard_map/all_gather | solution.py:115
  52.5 1.3 convert_reduce_fusion.1
  53.7 1.4 fusion.52
  55.9 1.5 fusion.46
  57.5 2.3 %convolution_convert_fusion.2 = bf16[32,32,256]{2,1,0:T(8,128)(2,1)} fusion(bf16[32,32,256]{2,1,0:T(8,128)(2,1)} %param.23, f32[256]{0:T(256)} %param.33, f32[32,32]{1,0:T(8,128)S(1)} %add_rsqrt_fusion.3, f32[32,32]{1,0:T(8,128)S(1)} %broadcast_multiply_fusion.3, bf16[256,256]{1,0:T(8,128)(2,1)} %param.34), kind=kOutput, calls=%fused_computation.56 | convolution fusion | flops 135790592 | bytes 1188864 | tf_op jit(solution)/shard_map/dot_general | solution.py:21
  59.8 10.4 %all_gather.15 = bf16[128,32,32]{2,1,0:T(8,128)(2,1)S(1)} all-gather(bf16[32,32,32]{2,1,0:T(8,128)(2,1)S(1)} %fusion.46), channel_id=1, replica_groups=mesh['seq'=8,'res'=4] {'res'}, dimensions={0}, use_global_device_ids=true | all-gather | bytes 327680 | tf_op jit(solution)/shard_map/all_gather | solution.py:114
  70.3 1.1 copy.90
  71.6 14.5 %all-gather.2.cloned.1.call-done = bf16[32,256,256]{2,1,0:T(8,128)(2,1)} async-done(((bf16[32,32,256]{2,1,0:T(8,128)(2,1)}), bf16[32,256,256]{2,1,0:T(8,128)(2,1)}) %all-gather.2.cloned.1.call-update) | async-done | bytes 4194320 | tf_op jit(solution)/shard_map/all_gather | solution.py:119
  86.0 3.5 %convert_reduce_fusion = f32[32,256]{1,0:T(8,128)S(1)} fusion(bf16[32,256,256]{2,1,0:T(8,128)(2,1)} %all-gather.2.cloned.1.call-done), kind=kLoop, calls=%fused_computation.28 | loop fusion | flops 4186112 | bytes 4227072 | tf_op jit(solution)/shard_map/reduce_sum | solution.py:14
  89.6 2.4 %fusion.23 = f32[32,256]{1,0:T(8,128)S(1)} fusion(bf16[32,256,256]{2,1,0:T(8,128)(2,1)S(1)} %copy-done.1, f32[32,256]{1,0:T(8,128)S(1)} %broadcast_multiply_fusion), kind=kLoop, calls=%fused_computation.35 | loop fusion | flops 8380416 | bytes 4259840 | tf_op jit(solution)/shard_map/reduce_sum | solution.py:15
  92.6 3.7 %fusion.41 = bf16[32,256,32]{1,2,0:T(8,128)(2,1)S(1)} fusion(bf16[32,256,256]{2,1,0:T(8,128)(2,1)S(1)} %copy-done.1, f32[256]{0:T(256)S(1)} %copy-done.20, f32[32,256]{1,0:T(8,128)S(1)} %add_rsqrt_fusion, f32[32,256]{1,0:T(8,128)S(1)} %broadcast_multiply_fusion, f32[32,256]{1,0:T(8,128)S(1)} %get-tuple-element.209, bf16[256,32]{0,1:T(8,128)(2,1)S(1)} %copy-done.19), kind=kOutput, calls=%fused_computation.57 | convolution fusion | flops 145227776 | bytes 4834304 | tf_op jit(solution)/shard_map/dot_general | solution.py:21
  96.4 3.0 %copy.86 = bf16[32,256,32]{2,0,1:T(8,128)(2,1)S(1)} copy(bf16[32,256,32]{1,2,0:T(8,128)(2,1)S(1)} %fusion.41) | data formatting | bytes 1048576 | tf_op jit(solution)/shard_map/convert_element_type | solution.py:127
  99.4 2.9 %reshape.185 = bf16[4,2,32768]{2,1,0:T(2,128)(2,1)} reshape(bf16[256,32,32]{2,1,0:T(8,128)(2,1)S(1)} %bitcast.151) | data formatting | bytes 1048576
  102.3 3.7 %all-to-all-start = ((bf16[4,2,32768]{2,1,0:T(2,128)(2,1)}), bf16[4,2,32768]{2,1,0:T(2,128)(2,1)S(1)}, u32[]{:S(2)}, u32[]{:S(2)}) async-start(bf16[4,2,32768]{2,1,0:T(2,128)(2,1)} %reshape.185), calls=%async_computation | async-start | bytes 1048576 | tf_op jit(solution)/shard_map/all_to_all | solution.py:129
  106.0 5.7 %convolution_convert_fusion.1 = bf16[32,256,256]{2,1,0:T(8,128)(2,1)} fusion(bf16[32,256,256]{2,1,0:T(8,128)(2,1)} %all-gather.2.cloned.1.call-done, f32[256]{0:T(256)} %param.33, f32[32,256]{1,0:T(8,128)} %copy-done.8, f32[32,256]{1,0:T(8,128)S(1)} %broadcast_multiply_fusion, bf16[256,256]{1,0:T(8,128)(2,1)} %param.36), kind=kOutput, calls=%fused_computation.42 | convolution fusion | flops 1086324736 | bytes 8586240 | tf_op jit(solution)/shard_map/dot_general | solution.py:21
  111.8 4.3 %convolution_convert_fusion = bf16[32,256,256]{2,1,0:T(8,128)(2,1)} fusion(bf16[32,256,256]{2,1,0:T(8,128)(2,1)S(1)} %copy-done.2, f32[256]{0:T(256)S(1)} %copy-done.21, f32[32,256]{1,0:T(8,128)S(1)} %copy-done.9, f32[32,256]{1,0:T(8,128)S(1)} %broadcast_multiply_fusion, bf16[256,256]{1,0:T(8,128)(2,1)S(1)} %copy-done.16), kind=kOutput, calls=%fused_computation.41 | convolution fusion | flops 1086324736 | bytes 8586240 | tf_op jit(solution)/shard_map/dot_general | solution.py:21
  116.1 1.1 reshape.186
  117.2 2.2 copy.121
  119.3 3.5 %reshape.165 = bf16[128,2048]{1,0:T(8,128)(2,1)S(1)} reshape(bf16[4,32,64,32]{3,2,1,0:T(8,128)(2,1)} %bitcast.153) | data formatting | bytes 1048576 | tf_op jit(solution)/shard_map/reshape | solution.py:133
  123.2 15.9 %while.22 = (s32[]{:T(128)}, f32[2,16,64,128]{3,2,1,0:T(8,128)}, s32[2]{0:T(128)S(1)}, bf16[128,32,32]{0,2,1:T(8,128)(2,1)S(1)}, bf16[128,2048]{0,1:T(8,128)(2,1...) while((s32[]{:T(128)}, f32[2,16,64,128]{3,2,1,0:T(8,128)}, ...), condition=%wide.region_5.0_spmd, body=%wide.region_4.0_spmd.sunk | while | flops 538313728 | bytes 9863843 | solution.py:159
  125.7 1.3 convert_bitcast_fusion.2
  127.0 1.8 copy.129
  129.0 2.1 fusion.126
  133.6 1.3 convert_bitcast_fusion.2
  134.9 1.8 copy.129
  137.0 2.1 fusion.126
  139.1 1.6 fusion.95
  142.6 7.7 %all_gather.19 = bf16[8,32,256]{1,0,2:T(8,128)(2,1)S(1)} all-gather(bf16[8,32,64]{1,0,2:T(8,128)(2,1)S(1)} %copy.92), channel_id=1, replica_groups=mesh['seq'=8,'res'=4] {'res'}, dimensions={2}, use_global_device_ids=true | all-gather | bytes 163840 | tf_op jit(solution)/shard_map/all_gather | solution.py:165
  150.6 60.1 %while.23 = (s32[]{:T(128)}, f32[4,8,32,256]{3,2,1,0:T(8,128)}, f32[4,8,32,8]{2,3,1,0:T(8,128)S(1)}, bf16[4,8,256,256]{3,2,1,0:T(8,128)(2,1)}, f32[4,8,256]{2,1,...) while((s32[]{:T(128)}, f32[4,8,32,256]{3,2,1,0:T(8,128)}, ...), condition=%wide.region_11.12_spmd, body=%wide.region_8.0_spmd.sunk | while | flops 71366656 | bytes 19509868 | solution.py:43
  150.6 2.7 %constant_dynamic-slice_fusion.5 = (bf16[1,8,256,256]{3,2,1,0:T(8,128)(2,1)S(1)}, bf16[1,8,256,256]{3,2,1,0:T(8,128)(2,1)}) fusion(bf16[4,8,256,256]{3,2,1,0:T(8,128)(2,1)} %get-tuple-element.375, s32[]{:T(128)} %get-tuple-element.360, bf16[4,8,256,256]{3,2,1,0:T(8,128)(2,1)} %get-tuple-element.372), kind=kLoop, calls=%fused_computation.24.clone.1 | loop fusion | bytes 4194308 | tf_op jit(solution)/shard_map/while/body/jit(dynamic_index_in_dim)/dynamic_slice | solution.py:43
  153.2 1.3 copy.132
  154.6 0.9 constant_dynamic-slice_fusion.6
  155.8 1.8 fusion.131
  158.3 2.3 %copy.131 = bf16[1,8,256,256]{2,3,1,0:T(8,128)(2,1)} copy(bf16[1,8,256,256]{3,2,1,0:T(8,128)(2,1)} %get-tuple-element.314) | data formatting | bytes 2097152 | tf_op jit(solution)/shard_map/while/body/jit(dynamic_index_in_dim)/dynamic_slice | solution.py:43
  160.6 2.7 %fusion.132 = f32[8,8,32,32]{3,2,1,0:T(8,128)} fusion(bf16[8,256,8,32]{1,3,2,0:T(8,128)(2,1)} %bitcast.149, f32[8,8,32,256]{3,2,1,0:T(8,128)S(1)} %get-tuple-element.316, f32[8,8,32]{2,1,0:T(8,128)S(1)} %get-tuple-element.317), kind=kOutput, calls=%fused_computation.17.clone.1 | convolution fusion | flops 34603008 | bytes 3416064 | tf_op jit(solution)/shard_map/while/body/eval_jaxpr/shij,sjhd->sihd/dot_general | solution.py:65
  163.3 1.5 copy.133
  165.6 2.7 %constant_dynamic-slice_fusion.5 = (bf16[1,8,256,256]{3,2,1,0:T(8,128)(2,1)S(1)}, bf16[1,8,256,256]{3,2,1,0:T(8,128)(2,1)}) fusion(bf16[4,8,256,256]{3,2,1,0:T(8,128)(2,1)} %get-tuple-element.375, s32[]{:T(128)} %get-tuple-element.360, bf16[4,8,256,256]{3,2,1,0:T(8,128)(2,1)} %get-tuple-element.372), kind=kLoop, calls=%fused_computation.24.clone.1 | loop fusion | bytes 4194308 | tf_op jit(solution)/shard_map/while/body/jit(dynamic_index_in_dim)/dynamic_slice | solution.py:43
  168.3 1.3 copy.132
  169.6 0.9 constant_dynamic-slice_fusion.6
  170.8 1.8 fusion.131
  173.3 2.3 %copy.131 = bf16[1,8,256,256]{2,3,1,0:T(8,128)(2,1)} copy(bf16[1,8,256,256]{3,2,1,0:T(8,128)(2,1)} %get-tuple-element.314) | data formatting | bytes 2097152 | tf_op jit(solution)/shard_map/while/body/jit(dynamic_index_in_dim)/dynamic_slice | solution.py:43
  175.6 2.7 %fusion.132 = f32[8,8,32,32]{3,2,1,0:T(8,128)} fusion(bf16[8,256,8,32]{1,3,2,0:T(8,128)(2,1)} %bitcast.149, f32[8,8,32,256]{3,2,1,0:T(8,128)S(1)} %get-tuple-element.316, f32[8,8,32]{2,1,0:T(8,128)S(1)} %get-tuple-element.317), kind=kOutput, calls=%fused_computation.17.clone.1 | convolution fusion | flops 34603008 | bytes 3416064 | tf_op jit(solution)/shard_map/while/body/eval_jaxpr/shij,sjhd->sihd/dot_general | solution.py:65
  178.4 1.5 copy.133
  180.6 2.7 %constant_dynamic-slice_fusion.5 = (bf16[1,8,256,256]{3,2,1,0:T(8,128)(2,1)S(1)}, bf16[1,8,256,256]{3,2,1,0:T(8,128)(2,1)}) fusion(bf16[4,8,256,256]{3,2,1,0:T(8,128)(2,1)} %get-tuple-element.375, s32[]{:T(128)} %get-tuple-element.360, bf16[4,8,256,256]{3,2,1,0:T(8,128)(2,1)} %get-tuple-element.372), kind=kLoop, calls=%fused_computation.24.clone.1 | loop fusion | bytes 4194308 | tf_op jit(solution)/shard_map/while/body/jit(dynamic_index_in_dim)/dynamic_slice | solution.py:43
  183.3 1.3 copy.132
  184.7 0.9 constant_dynamic-slice_fusion.6
  185.9 1.8 fusion.131
  188.3 2.3 %copy.131 = bf16[1,8,256,256]{2,3,1,0:T(8,128)(2,1)} copy(bf16[1,8,256,256]{3,2,1,0:T(8,128)(2,1)} %get-tuple-element.314) | data formatting | bytes 2097152 | tf_op jit(solution)/shard_map/while/body/jit(dynamic_index_in_dim)/dynamic_slice | solution.py:43
  190.7 2.7 %fusion.132 = f32[8,8,32,32]{3,2,1,0:T(8,128)} fusion(bf16[8,256,8,32]{1,3,2,0:T(8,128)(2,1)} %bitcast.149, f32[8,8,32,256]{3,2,1,0:T(8,128)S(1)} %get-tuple-element.316, f32[8,8,32]{2,1,0:T(8,128)S(1)} %get-tuple-element.317), kind=kOutput, calls=%fused_computation.17.clone.1 | convolution fusion | flops 34603008 | bytes 3416064 | tf_op jit(solution)/shard_map/while/body/eval_jaxpr/shij,sjhd->sihd/dot_general | solution.py:65
  193.4 1.5 copy.133
  195.7 2.7 %constant_dynamic-slice_fusion.5 = (bf16[1,8,256,256]{3,2,1,0:T(8,128)(2,1)S(1)}, bf16[1,8,256,256]{3,2,1,0:T(8,128)(2,1)}) fusion(bf16[4,8,256,256]{3,2,1,0:T(8,128)(2,1)} %get-tuple-element.375, s32[]{:T(128)} %get-tuple-element.360, bf16[4,8,256,256]{3,2,1,0:T(8,128)(2,1)} %get-tuple-element.372), kind=kLoop, calls=%fused_computation.24.clone.1 | loop fusion | bytes 4194308 | tf_op jit(solution)/shard_map/while/body/jit(dynamic_index_in_dim)/dynamic_slice | solution.py:43
  198.3 1.3 copy.132
  199.7 0.9 constant_dynamic-slice_fusion.6
  200.9 1.8 fusion.131
  203.4 2.3 %copy.131 = bf16[1,8,256,256]{2,3,1,0:T(8,128)(2,1)} copy(bf16[1,8,256,256]{3,2,1,0:T(8,128)(2,1)} %get-tuple-element.314) | data formatting | bytes 2097152 | tf_op jit(solution)/shard_map/while/body/jit(dynamic_index_in_dim)/dynamic_slice | solution.py:43
  205.7 2.7 %fusion.132 = f32[8,8,32,32]{3,2,1,0:T(8,128)} fusion(bf16[8,256,8,32]{1,3,2,0:T(8,128)(2,1)} %bitcast.149, f32[8,8,32,256]{3,2,1,0:T(8,128)S(1)} %get-tuple-element.316, f32[8,8,32]{2,1,0:T(8,128)S(1)} %get-tuple-element.317), kind=kOutput, calls=%fused_computation.17.clone.1 | convolution fusion | flops 34603008 | bytes 3416064 | tf_op jit(solution)/shard_map/while/body/eval_jaxpr/shij,sjhd->sihd/dot_general | solution.py:65
  208.4 1.5 copy.133
  210.9 2.6 %div.59 = f32[32,32,8,32]{3,2,1,0:T(8,128)} broadcast(f32[32,32,8]{2,1,0:T(8,128)S(1)} %copy.97), dimensions={0,1,2} | broadcast | bytes 1081344 | tf_op jit(solution)/shard_map/div | solution.py:179
  213.5 3.4 %div.60 = f32[32,32,256]{2,1,0:T(8,128)S(1)} reshape(f32[32,32,8,32]{3,2,1,0:T(8,128)} %div.59) | data formatting | bytes 2097152 | tf_op jit(solution)/shard_map/div | solution.py:179
  216.9 1.1 bitcast_divide_fusion
  218.1 2.0 fusion.97
  220.6 2.4 %fusion.39 = f32[32,32,256]{2,1,0:T(8,128)} fusion(f32[32,32,256]{2,1,0:T(8,128)S(1)} %get-tuple-element.211, bf16[1024,256]{1,0:T(8,128)(2,1)S(1)} %copy-done, bf16[256,1024]{1,0:T(8,128)(2,1)S(1)} %copy-done.14, f32[256]{0:T(256)S(1)} %copy-done.23, f32[32,32]{1,0:T(8,128)S(1)} %add_rsqrt_fusion.1, f32[32,32]{1,0:T(8,128)S(1)} %broadcast_multiply_fusion.2), kind=kOutput, calls=%fused_computation.54 | convolution fusion | flops 1077149696 | bytes 3154944 | tf_op jit(solution)/shard_map/dot_general | solution.py:21
  (115 shorter events, 16.8 us)
Async XLA Ops:
  7.2 213.4 %copy-start = (bf16[1024,256]{1,0:T(8,128)(2,1)S(1)}, bf16[1024,256]{1,0:T(8,128)(2,1)}, u32[]{:S(2)}) copy-start(bf16[1024,256]{1,0:T(8,128)(2,1)} %param.41) | copy-start | bytes 1572868
  7.2 78.9 %all-gather.2.cloned.1.call-start = ((), (), s32[]{:S(2)}) async-start(), calls=%async_computation.2 | async-start | bytes 4718592 | tf_op jit(solution)/shard_map/all_gather | solution.py:119
  42.4 29.0 %all-to-all-start.1 = ((bf16[4,2,1024]{2,1,0:T(2,128)(2,1)}), bf16[4,2,1024]{2,1,0:T(2,128)(2,1)S(1)}, u32[]{:S(2)}, u32[]{:S(2)}) async-start(bf16[4,2,1024]{2,1,0:T(2,128)(2,1)} %reshape.187), calls=%async_computation.1 | async-start | bytes 32768 | tf_op jit(solution)/shard_map/all_to_all | solution.py:130
  55.2 2.3 %copy-start.10 = (f32[32,32]{1,0:T(8,128)}, f32[32,32]{1,0:T(8,128)S(1)}, u32[]{:S(2)}) copy-start(f32[32,32]{1,0:T(8,128)S(1)} %add_rsqrt_fusion.3) | copy-start | bytes 12292
  71.5 21.1 %copy-start.19 = (bf16[256,32]{0,1:T(8,128)(2,1)S(1)}, bf16[256,32]{0,1:T(8,128)(2,1)}, u32[]{:S(2)}) copy-start(bf16[256,32]{0,1:T(8,128)(2,1)} %param.29) | copy-start | bytes 49156
  71.6 21.1 %copy-start.20 = (f32[256]{0:T(256)S(1)}, f32[256]{0:T(256)}, u32[]{:S(2)}) copy-start(f32[256]{0:T(256)} %param.27) | copy-start | bytes 3076
  86.0 3.5 %copy-start.1 = (bf16[32,256,256]{2,1,0:T(8,128)(2,1)S(1)}, bf16[32,256,256]{2,1,0:T(8,128)(2,1)}, u32[]{:S(2)}) copy-start(bf16[32,256,256]{2,1,0:T(8,128)(2,1)} %all-gather.2.cloned.1.call-done) | copy-start | bytes 12582916
  92.0 0.6 copy-start.8
  102.3 13.7 %all-to-all-start = ((bf16[4,2,32768]{2,1,0:T(2,128)(2,1)}), bf16[4,2,32768]{2,1,0:T(2,128)(2,1)S(1)}, u32[]{:S(2)}, u32[]{:S(2)}) async-start(bf16[4,2,32768]{2,1,0:T(2,128)(2,1)} %reshape.185), calls=%async_computation | async-start | bytes 1048576 | tf_op jit(solution)/shard_map/all_to_all | solution.py:129
  106.0 5.8 %copy-start.2 = (bf16[32,256,256]{2,1,0:T(8,128)(2,1)S(1)}, bf16[32,256,256]{2,1,0:T(8,128)(2,1)}, u32[]{:S(2)}) copy-start(bf16[32,256,256]{2,1,0:T(8,128)(2,1)} %all-gather.2.cloned.1.call-done) | copy-start | bytes 12582916
  106.0 5.7 %copy-start.9 = (f32[32,256]{1,0:T(8,128)S(1)}, f32[32,256]{1,0:T(8,128)}, u32[]{:S(2)}) copy-start(f32[32,256]{1,0:T(8,128)} %copy-done.8) | copy-start | bytes 98308
  106.0 5.7 %copy-start.16 = (bf16[256,256]{1,0:T(8,128)(2,1)S(1)}, bf16[256,256]{1,0:T(8,128)(2,1)}, u32[]{:S(2)}) copy-start(bf16[256,256]{1,0:T(8,128)(2,1)} %param.35) | copy-start | bytes 393220
  106.0 5.7 %copy-start.21 = (f32[256]{0:T(256)S(1)}, f32[256]{0:T(256)}, u32[]{:S(2)}) copy-start(f32[256]{0:T(256)} %param.33) | copy-start | bytes 3076
  117.1 6.0 %copy-start.15 = (bf16[1024,128]{1,0:T(8,128)(2,1)S(1)}, bf16[1024,128]{1,0:T(8,128)(2,1)}, u32[]{:S(2)}) copy-start(bf16[1024,128]{1,0:T(8,128)(2,1)} %param.30) | copy-start | bytes 786436
  117.2 6.0 %copy-start.24 = (s32[2]{0:T(128)S(1)}, s32[2]{0:T(128)}, u32[]{:S(2)}) copy-start(s32[2]{0:T(128)} %iota_multiply_fusion) | copy-start | bytes 28
  123.1 15.9 %copy-start.5 = (f32[32,64,128]{2,1,0:T(8,128)S(1)}, f32[32,64,128]{2,1,0:T(8,128)}, u32[]{:S(2)}) copy-start(f32[32,64,128]{2,1,0:T(8,128)} %param.26) | copy-start | bytes 3145732
  139.1 2.6 %copy-start.12 = (bf16[128,8]{0,1:T(8,128)(2,1)S(1)}, bf16[128,8]{0,1:T(8,128)(2,1)}, u32[]{:S(2)}) copy-start(bf16[128,8]{0,1:T(8,128)(2,1)} %param.32) | copy-start | bytes 6148
  139.1 2.6 %copy-start.13 = (f32[128]{0:T(128)S(1)}, f32[128]{0:T(128)}, u32[]{:S(2)}) copy-start(f32[128]{0:T(128)} %param.31) | copy-start | bytes 1540
  139.1 11.5 %copy-start.7 = (f32[4,8,32,8]{2,3,1,0:T(8,128)S(1)}, f32[4,8,32,8]{2,3,1,0:T(8,128)}, u32[]{:S(2)}) copy-start(f32[4,8,32,8]{2,3,1,0:T(8,128)} %custom-call.2) | copy-start | bytes 98308
  140.7 1.0 copy-start.3
  210.9 6.0 %copy-start.6 = (f32[4,8,32,256]{3,2,1,0:T(8,128)S(1)}, f32[4,8,32,256]{3,2,1,0:T(8,128)}, u32[]{:S(2)}) copy-start(f32[4,8,32,256]{3,2,1,0:T(8,128)} %get-tuple-element.88) | copy-start | bytes 3145732
  213.5 4.6 %copy-start.4 = (bf16[32,32,256]{2,1,0:T(8,128)(2,1)S(1)}, bf16[32,32,256]{2,1,0:T(8,128)(2,1)}, u32[]{:S(2)}) copy-start(bf16[32,32,256]{2,1,0:T(8,128)(2,1)} %param.23) | copy-start | bytes 1572868
  213.5 4.6 %copy-start.11 = (f32[32,32]{1,0:T(8,128)S(1)}, f32[32,32]{1,0:T(8,128)}, u32[]{:S(2)}) copy-start(f32[32,32]{1,0:T(8,128)} %copy-done.10) | copy-start | bytes 12292
  213.5 4.6 %copy-start.17 = (bf16[256,256]{1,0:T(8,128)(2,1)S(1)}, bf16[256,256]{1,0:T(8,128)(2,1)}, u32[]{:S(2)}) copy-start(bf16[256,256]{1,0:T(8,128)(2,1)} %param.38) | copy-start | bytes 393220
  213.5 4.6 %copy-start.18 = (bf16[256,256]{1,0:T(8,128)(2,1)S(1)}, bf16[256,256]{1,0:T(8,128)(2,1)}, u32[]{:S(2)}) copy-start(bf16[256,256]{1,0:T(8,128)(2,1)} %param.37) | copy-start | bytes 393220
  213.5 4.6 %copy-start.22 = (f32[256]{0:T(256)S(1)}, f32[256]{0:T(256)}, u32[]{:S(2)}) copy-start(f32[256]{0:T(256)} %param.33) | copy-start | bytes 3076
  218.1 2.4 %copy-start.14 = (bf16[256,1024]{1,0:T(8,128)(2,1)S(1)}, bf16[256,1024]{1,0:T(8,128)(2,1)}, u32[]{:S(2)}) copy-start(bf16[256,1024]{1,0:T(8,128)(2,1)} %param.40) | copy-start | bytes 1572868
  218.1 2.4 %copy-start.23 = (f32[256]{0:T(256)S(1)}, f32[256]{0:T(256)}, u32[]{:S(2)}) copy-start(f32[256]{0:T(256)} %param.39) | copy-start | bytes 3076
Sparse Core Ops, SparseCore 0:
  10.2 75.8 all-gather.1
where the time goes:
time: 231 us; the launch traced here: 230 us
  local copies, waits for them, and re-layouts  67.4 us (29%)
  blocking collectives  56.3 us (24%)
  matrix products  48.2 us (21%)
  other arithmetic  17.2 us (7%)
  waiting for transfers between devices  15.2 us (7%)
  between operations  14.5 us (6%)
  starting transfers between devices  6.94 us (3%)
  loops' own time  4.13 us (2%)
    all_gather x1, blocking collectives, on_device(): lax.all_gather(mask_local, 'seq', axis=1, tiled=True)  32.9 us
    dynamic_slice x16, local copies, waits for them, and re-layouts, in_blocks(): outputs = lax.map(function, shaped)  28.9 us
    dot_general x7, matrix products, project(): result = jnp.dot(flattened, weight, preferred_element_type=jnp.float32)  22 us
    all_gather x1, waiting for transfers between devices, on_device(): lax.all_gather(alignment, 'seq', axis=1, tiled=True)  14.5 us
    dot_general x4, matrix products, head_weigh(): jnp.einsum('shij,sjhd->sihd', weights.astype(jnp.bfloat16), values.reshap...  10.9 us
    all_gather x1, blocking collectives, on_device(): lax.all_gather(left_local, 'res', axis=0, tiled=True)  10.4 us
    dynamic_update_slice x12, local copies, waits for them, and re-layouts, in_blocks(): outputs = lax.map(function, shaped)  9.08 us
    all_gather x1, blocking collectives, on_device(): full_bias = lax.all_gather(pair_bias, 'res', axis=2, tiled=True)  7.68 us
  transfers between devices with their start and end apart: 3, of which 1 were waited for; matrix products, arithmetic and copies ran while one was open for 9% of the time, Pallas kernels for 0%

commit v1 on v0

--- a/solution.py
+++ b/solution.py
@@ -117,7 +117,7 @@
     row_flags = (row_mask.astype(jnp.float32) * row_live[None, :]).astype(jnp.bfloat16)
     wide_alignment, wide_mask = (
         lax.all_gather(alignment, "seq", axis=1, tiled=True),
-        lax.all_gather(mask_local, "seq", axis=1, tiled=True),
+        jnp.concatenate(lax.all_gather(mask_local, "seq"), axis=1),
     )
     wide_live = wide_mask.astype(jnp.float32) * residue_live[None, :]
     key_norm = layer_norm(wide_alignment, row_gain).astype(jnp.bfloat16)

time: 231 us -> 231 us (level)
    unnamed x55 -> x60, local copies, waits for them, and re-layouts: 6.6 us -> 5.84 us
where the time goes in v1:
time: 231 us; the launch traced here: 230 us
  local copies, waits for them, and re-layouts  66.7 us (29%)
  blocking collectives  56.3 us (24%)
  matrix products  47.2 us (20%)
  other arithmetic  17.9 us (8%)
  waiting for transfers between devices  16.3 us (7%)
  between operations  14.6 us (6%)
  starting transfers between devices  6.94 us (3%)
  loops' own time  4.13 us (2%)
    all_gather x1, blocking collectives, on_device(): lax.all_gather(mask_local, 'seq')  32.9 us
    dynamic_slice x16, local copies, waits for them, and re-layouts, in_blocks(): outputs = lax.map(function, shaped)  29 us
    dot_general x7, matrix products, project(): result = jnp.dot(flattened, weight, preferred_element_type=jnp.float32)  21 us
    all_gather x1, waiting for transfers between devices, on_device(): lax.all_gather(alignment, 'seq', axis=1, tiled=True)  15.6 us
    dot_general x4, matrix products, head_weigh(): jnp.einsum('shij,sjhd->sihd', weights.astype(jnp.bfloat16), values.reshap...  10.9 us
    all_gather x1, blocking collectives, on_device(): lax.all_gather(left_local, 'res', axis=0, tiled=True)  10.4 us
    dynamic_update_slice x12, local copies, waits for them, and re-layouts, in_blocks(): outputs = lax.map(function, shaped)  9.1 us
    all_gather x1, blocking collectives, on_device(): full_bias = lax.all_gather(pair_bias, 'res', axis=2, tiled=True)  7.68 us
  transfers between devices with their start and end apart: 3, of which 1 were waited for; matrix products, arithmetic and copies ran while one was open for 9% of the time, Pallas kernels for 0%

profile of v1, /device:TPU:0, one launch (start us, length us, event | category | flops | bytes accessed | tf_op | source)
XLA Modules:
  0.0 230.0 jit_solution(16668505693018412719)
XLA Ops:
  8.7 32.9 %all-gather = bf16[256,32]{1,0:T(8,128)(2,1)S(1)} all-gather(bf16[32,32]{1,0:T(8,128)(2,1)S(1)} %convert_element_type.124), channel_id=2, replica_groups=mesh['seq'=8,'res'=4] {'seq'}, dimensions={0}, use_global_device_ids=true | all-gather | bytes 18432 | tf_op jit(solution)/shard_map/all_gather | solution.py:120
  42.5 3.3 %all-to-all-start.1 = ((bf16[4,2,1024]{2,1,0:T(2,128)(2,1)}), bf16[4,2,1024]{2,1,0:T(2,128)(2,1)S(1)}, u32[]{:S(2)}, u32[]{:S(2)}) async-start(bf16[4,2,1024]{2,1,0:T(2,128)(2,1)} %reshape.217), calls=%async_computation.1 | async-start | bytes 32768 | tf_op jit(solution)/shard_map/all_to_all | solution.py:130
  46.7 5.2 %all_gather.22 = bf16[128,32]{1,0:T(8,128)(2,1)S(1)} all-gather(bf16[32,32]{1,0:T(8,128)(2,1)S(1)} %convert_element_type.124), channel_id=1, replica_groups=mesh['seq'=8,'res'=4] {'res'}, dimensions={0}, use_global_device_ids=true | all-gather | bytes 10240 | tf_op jit(solution)/shard_map/all_gather | solution.py:115
  52.4 1.3 convert_reduce_fusion.1
  53.7 1.4 fusion.52
  55.9 1.5 fusion.46
  57.5 1.3 convolution_convert_fusion.2
  58.8 10.4 %all_gather.18 = bf16[128,32,32]{2,1,0:T(8,128)(2,1)S(1)} all-gather(bf16[32,32,32]{2,1,0:T(8,128)(2,1)S(1)} %fusion.46), channel_id=1, replica_groups=mesh['seq'=8,'res'=4] {'res'}, dimensions={0}, use_global_device_ids=true | all-gather | bytes 327680 | tf_op jit(solution)/shard_map/all_gather | solution.py:114
  69.2 1.1 copy.53
  70.5 15.6 %all-gather.3.cloned.1.call-done = bf16[32,256,256]{2,1,0:T(8,128)(2,1)} async-done(((bf16[32,32,256]{2,1,0:T(8,128)(2,1)}), bf16[32,256,256]{2,1,0:T(8,128)(2,1)}) %all-gather.3.cloned.1.call-update) | async-done | bytes 4194320 | tf_op jit(solution)/shard_map/all_gather | solution.py:119
  86.1 3.5 %convert_reduce_fusion = f32[32,256]{1,0:T(8,128)S(1)} fusion(bf16[32,256,256]{2,1,0:T(8,128)(2,1)} %all-gather.3.cloned.1.call-done), kind=kLoop, calls=%fused_computation.28 | loop fusion | flops 4186112 | bytes 4227072 | tf_op jit(solution)/shard_map/reduce_sum | solution.py:14
  89.6 2.4 %fusion.23 = f32[32,256]{1,0:T(8,128)S(1)} fusion(bf16[32,256,256]{2,1,0:T(8,128)(2,1)S(1)} %copy-done.1, f32[32,256]{1,0:T(8,128)S(1)} %broadcast_multiply_fusion.2), kind=kLoop, calls=%fused_computation.35 | loop fusion | flops 8380416 | bytes 4259840 | tf_op jit(solution)/shard_map/reduce_sum | solution.py:15
  92.7 3.7 %fusion.41 = bf16[32,256,32]{1,2,0:T(8,128)(2,1)S(1)} fusion(bf16[32,256,256]{2,1,0:T(8,128)(2,1)S(1)} %copy-done.1, f32[256]{0:T(256)S(1)} %copy-done.22, f32[32,256]{1,0:T(8,128)S(1)} %add_rsqrt_fusion, f32[32,256]{1,0:T(8,128)S(1)} %broadcast_multiply_fusion.2, f32[32,256]{1,0:T(8,128)S(1)} %broadcast_multiply_fusion.1, bf16[256,32]{0,1:T(8,128)(2,1)S(1)} %copy-done.21), kind=kOutput, calls=%fused_computation.57 | convolution fusion | flops 145227776 | bytes 4834304 | tf_op jit(solution)/shard_map/dot_general | solution.py:21
  96.4 3.0 %copy.50 = bf16[32,256,32]{2,0,1:T(8,128)(2,1)S(1)} copy(bf16[32,256,32]{1,2,0:T(8,128)(2,1)S(1)} %fusion.41) | data formatting | bytes 1048576 | tf_op jit(solution)/shard_map/convert_element_type | solution.py:127
  99.5 2.9 %reshape.215 = bf16[4,2,32768]{2,1,0:T(2,128)(2,1)} reshape(bf16[256,32,32]{2,1,0:T(8,128)(2,1)S(1)} %bitcast.155) | data formatting | bytes 1048576
  102.4 3.7 %all-to-all-start = ((bf16[4,2,32768]{2,1,0:T(2,128)(2,1)}), bf16[4,2,32768]{2,1,0:T(2,128)(2,1)S(1)}, u32[]{:S(2)}, u32[]{:S(2)}) async-start(bf16[4,2,32768]{2,1,0:T(2,128)(2,1)} %reshape.215), calls=%async_computation | async-start | bytes 1048576 | tf_op jit(solution)/shard_map/all_to_all | solution.py:129
  106.1 5.7 %convolution_convert_fusion.1 = bf16[32,256,256]{2,1,0:T(8,128)(2,1)} fusion(bf16[32,256,256]{2,1,0:T(8,128)(2,1)} %all-gather.3.cloned.1.call-done, f32[256]{0:T(256)} %param.33, f32[32,256]{1,0:T(8,128)} %copy-done.9, f32[32,256]{1,0:T(8,128)S(1)} %broadcast_multiply_fusion.2, bf16[256,256]{1,0:T(8,128)(2,1)} %param.36), kind=kOutput, calls=%fused_computation.42 | convolution fusion | flops 1086324736 | bytes 8586240 | tf_op jit(solution)/shard_map/dot_general | solution.py:21
  111.8 4.4 %convolution_convert_fusion = bf16[32,256,256]{2,1,0:T(8,128)(2,1)} fusion(bf16[32,256,256]{2,1,0:T(8,128)(2,1)S(1)} %copy-done.2, f32[256]{0:T(256)S(1)} %copy-done.24, f32[32,256]{1,0:T(8,128)S(1)} %copy-done.10, f32[32,256]{1,0:T(8,128)S(1)} %broadcast_multiply_fusion.2, bf16[256,256]{1,0:T(8,128)(2,1)S(1)} %copy-done.18), kind=kOutput, calls=%fused_computation.41 | convolution fusion | flops 1086324736 | bytes 8586240 | tf_op jit(solution)/shard_map/dot_general | solution.py:21
  116.2 1.1 reshape.216
  117.3 2.2 copy.88
  119.5 3.5 %reshape.193 = bf16[128,2048]{1,0:T(8,128)(2,1)S(1)} reshape(bf16[4,32,64,32]{3,2,1,0:T(8,128)(2,1)} %bitcast.157) | data formatting | bytes 1048576 | tf_op jit(solution)/shard_map/reshape | solution.py:133
  123.3 15.9 %while.22 = (s32[]{:T(128)}, f32[2,16,64,128]{3,2,1,0:T(8,128)}, s32[2]{0:T(128)S(1)}, bf16[128,32,32]{0,2,1:T(8,128)(2,1)S(1)}, bf16[128,2048]{0,1:T(8,128)(2,1...) while((s32[]{:T(128)}, f32[2,16,64,128]{3,2,1,0:T(8,128)}, ...), condition=%wide.region_5.0_spmd, body=%wide.region_4.0_spmd.sunk | while | flops 538313728 | bytes 9863843 | solution.py:159
  125.9 1.3 convert_bitcast_fusion.2
  127.2 1.8 copy.97
  129.2 2.1 fusion.126
  133.8 1.3 convert_bitcast_fusion.2
  135.1 1.8 copy.97
  137.1 2.1 fusion.126
  139.2 1.6 fusion.95
  142.7 7.7 %all_gather.23 = bf16[8,32,256]{1,0,2:T(8,128)(2,1)S(1)} all-gather(bf16[8,32,64]{1,0,2:T(8,128)(2,1)S(1)} %copy.55), channel_id=1, replica_groups=mesh['seq'=8,'res'=4] {'res'}, dimensions={2}, use_global_device_ids=true | all-gather | bytes 163840 | tf_op jit(solution)/shard_map/all_gather | solution.py:165
  150.7 60.2 %while.23 = (s32[]{:T(128)}, f32[4,8,32,256]{3,2,1,0:T(8,128)}, f32[4,8,32,8]{2,3,1,0:T(8,128)S(1)}, bf16[4,8,256,256]{3,2,1,0:T(8,128)(2,1)}, f32[4,8,256]{2,1,...) while((s32[]{:T(128)}, f32[4,8,32,256]{3,2,1,0:T(8,128)}, ...), condition=%wide.region_11.12_spmd, body=%wide.region_8.0_spmd.sunk | while | flops 71366656 | bytes 19509868 | solution.py:43
  150.7 2.7 %constant_dynamic-slice_fusion.5 = (bf16[1,8,256,256]{3,2,1,0:T(8,128)(2,1)S(1)}, bf16[1,8,256,256]{3,2,1,0:T(8,128)(2,1)}) fusion(bf16[4,8,256,256]{3,2,1,0:T(8,128)(2,1)} %get-tuple-element.343, s32[]{:T(128)} %get-tuple-element.328, bf16[4,8,256,256]{3,2,1,0:T(8,128)(2,1)} %get-tuple-element.340), kind=kLoop, calls=%fused_computation.24.clone.1 | loop fusion | bytes 4194308 | tf_op jit(solution)/shard_map/while/body/jit(dynamic_index_in_dim)/dynamic_slice | solution.py:43
  153.4 1.3 copy.100
  154.8 0.9 constant_dynamic-slice_fusion.6
  156.0 1.8 fusion.131
  158.5 2.3 %copy.99 = bf16[1,8,256,256]{2,3,1,0:T(8,128)(2,1)} copy(bf16[1,8,256,256]{3,2,1,0:T(8,128)(2,1)} %get-tuple-element.282) | data formatting | bytes 2097152 | tf_op jit(solution)/shard_map/while/body/jit(dynamic_index_in_dim)/dynamic_slice | solution.py:43
  160.8 2.7 %fusion.132 = f32[8,8,32,32]{3,2,1,0:T(8,128)} fusion(bf16[8,256,8,32]{1,3,2,0:T(8,128)(2,1)} %bitcast.153, f32[8,8,32,256]{3,2,1,0:T(8,128)S(1)} %get-tuple-element.284, f32[8,8,32]{2,1,0:T(8,128)S(1)} %get-tuple-element.285), kind=kOutput, calls=%fused_computation.17.clone.1 | convolution fusion | flops 34603008 | bytes 3416064 | tf_op jit(solution)/shard_map/while/body/eval_jaxpr/shij,sjhd->sihd/dot_general | solution.py:65
  163.5 1.5 copy.101
  165.8 2.7 %constant_dynamic-slice_fusion.5 = (bf16[1,8,256,256]{3,2,1,0:T(8,128)(2,1)S(1)}, bf16[1,8,256,256]{3,2,1,0:T(8,128)(2,1)}) fusion(bf16[4,8,256,256]{3,2,1,0:T(8,128)(2,1)} %get-tuple-element.343, s32[]{:T(128)} %get-tuple-element.328, bf16[4,8,256,256]{3,2,1,0:T(8,128)(2,1)} %get-tuple-element.340), kind=kLoop, calls=%fused_computation.24.clone.1 | loop fusion | bytes 4194308 | tf_op jit(solution)/shard_map/while/body/jit(dynamic_index_in_dim)/dynamic_slice | solution.py:43
  168.5 1.3 copy.100
  169.8 0.9 constant_dynamic-slice_fusion.6
  171.0 1.8 fusion.131
  173.5 2.3 %copy.99 = bf16[1,8,256,256]{2,3,1,0:T(8,128)(2,1)} copy(bf16[1,8,256,256]{3,2,1,0:T(8,128)(2,1)} %get-tuple-element.282) | data formatting | bytes 2097152 | tf_op jit(solution)/shard_map/while/body/jit(dynamic_index_in_dim)/dynamic_slice | solution.py:43
  175.8 2.7 %fusion.132 = f32[8,8,32,32]{3,2,1,0:T(8,128)} fusion(bf16[8,256,8,32]{1,3,2,0:T(8,128)(2,1)} %bitcast.153, f32[8,8,32,256]{3,2,1,0:T(8,128)S(1)} %get-tuple-element.284, f32[8,8,32]{2,1,0:T(8,128)S(1)} %get-tuple-element.285), kind=kOutput, calls=%fused_computation.17.clone.1 | convolution fusion | flops 34603008 | bytes 3416064 | tf_op jit(solution)/shard_map/while/body/eval_jaxpr/shij,sjhd->sihd/dot_general | solution.py:65
  178.6 1.5 copy.101
  180.8 2.7 %constant_dynamic-slice_fusion.5 = (bf16[1,8,256,256]{3,2,1,0:T(8,128)(2,1)S(1)}, bf16[1,8,256,256]{3,2,1,0:T(8,128)(2,1)}) fusion(bf16[4,8,256,256]{3,2,1,0:T(8,128)(2,1)} %get-tuple-element.343, s32[]{:T(128)} %get-tuple-element.328, bf16[4,8,256,256]{3,2,1,0:T(8,128)(2,1)} %get-tuple-element.340), kind=kLoop, calls=%fused_computation.24.clone.1 | loop fusion | bytes 4194308 | tf_op jit(solution)/shard_map/while/body/jit(dynamic_index_in_dim)/dynamic_slice | solution.py:43
  183.5 1.3 copy.100
  184.8 0.9 constant_dynamic-slice_fusion.6
  186.0 1.8 fusion.131
  188.5 2.3 %copy.99 = bf16[1,8,256,256]{2,3,1,0:T(8,128)(2,1)} copy(bf16[1,8,256,256]{3,2,1,0:T(8,128)(2,1)} %get-tuple-element.282) | data formatting | bytes 2097152 | tf_op jit(solution)/shard_map/while/body/jit(dynamic_index_in_dim)/dynamic_slice | solution.py:43
  190.9 2.7 %fusion.132 = f32[8,8,32,32]{3,2,1,0:T(8,128)} fusion(bf16[8,256,8,32]{1,3,2,0:T(8,128)(2,1)} %bitcast.153, f32[8,8,32,256]{3,2,1,0:T(8,128)S(1)} %get-tuple-element.284, f32[8,8,32]{2,1,0:T(8,128)S(1)} %get-tuple-element.285), kind=kOutput, calls=%fused_computation.17.clone.1 | convolution fusion | flops 34603008 | bytes 3416064 | tf_op jit(solution)/shard_map/while/body/eval_jaxpr/shij,sjhd->sihd/dot_general | solution.py:65
  193.6 1.5 copy.101
  195.8 2.7 %constant_dynamic-slice_fusion.5 = (bf16[1,8,256,256]{3,2,1,0:T(8,128)(2,1)S(1)}, bf16[1,8,256,256]{3,2,1,0:T(8,128)(2,1)}) fusion(bf16[4,8,256,256]{3,2,1,0:T(8,128)(2,1)} %get-tuple-element.343, s32[]{:T(128)} %get-tuple-element.328, bf16[4,8,256,256]{3,2,1,0:T(8,128)(2,1)} %get-tuple-element.340), kind=kLoop, calls=%fused_computation.24.clone.1 | loop fusion | bytes 4194308 | tf_op jit(solution)/shard_map/while/body/jit(dynamic_index_in_dim)/dynamic_slice | solution.py:43
  198.5 1.3 copy.100
  199.9 0.9 constant_dynamic-slice_fusion.6
  201.1 1.8 fusion.131
  203.6 2.3 %copy.99 = bf16[1,8,256,256]{2,3,1,0:T(8,128)(2,1)} copy(bf16[1,8,256,256]{3,2,1,0:T(8,128)(2,1)} %get-tuple-element.282) | data formatting | bytes 2097152 | tf_op jit(solution)/shard_map/while/body/jit(dynamic_index_in_dim)/dynamic_slice | solution.py:43
  205.9 2.7 %fusion.132 = f32[8,8,32,32]{3,2,1,0:T(8,128)} fusion(bf16[8,256,8,32]{1,3,2,0:T(8,128)(2,1)} %bitcast.153, f32[8,8,32,256]{3,2,1,0:T(8,128)S(1)} %get-tuple-element.284, f32[8,8,32]{2,1,0:T(8,128)S(1)} %get-tuple-element.285), kind=kOutput, calls=%fused_computation.17.clone.1 | convolution fusion | flops 34603008 | bytes 3416064 | tf_op jit(solution)/shard_map/while/body/eval_jaxpr/shij,sjhd->sihd/dot_general | solution.py:65
  208.6 1.5 copy.101
  211.1 2.6 %div.59 = f32[32,32,8,32]{3,2,1,0:T(8,128)} broadcast(f32[32,32,8]{2,1,0:T(8,128)S(1)} %copy.60), dimensions={0,1,2} | broadcast | bytes 1081344 | tf_op jit(solution)/shard_map/div | solution.py:179
  213.7 3.4 %div.60 = f32[32,32,256]{2,1,0:T(8,128)S(1)} reshape(f32[32,32,8,32]{3,2,1,0:T(8,128)} %div.59) | data formatting | bytes 2097152 | tf_op jit(solution)/shard_map/div | solution.py:179
  217.1 1.1 bitcast_divide_fusion
  218.3 2.0 fusion.97
  220.8 2.4 %fusion.39 = f32[32,32,256]{2,1,0:T(8,128)} fusion(f32[32,32,256]{2,1,0:T(8,128)S(1)} %get-tuple-element.179, bf16[1024,256]{1,0:T(8,128)(2,1)S(1)} %copy-done, bf16[256,1024]{1,0:T(8,128)(2,1)S(1)} %copy-done.15, f32[256]{0:T(256)S(1)} %copy-done.26, f32[32,32]{1,0:T(8,128)S(1)} %add_rsqrt_fusion.1, f32[32,32]{1,0:T(8,128)S(1)} %broadcast_multiply_fusion.4), kind=kOutput, calls=%fused_computation.54 | convolution fusion | flops 1077149696 | bytes 3154944 | tf_op jit(solution)/shard_map/dot_general | solution.py:21
  (123 shorter events, 16.8 us)
Async XLA Ops:
  7.2 213.6 %copy-start = (bf16[1024,256]{1,0:T(8,128)(2,1)S(1)}, bf16[1024,256]{1,0:T(8,128)(2,1)}, u32[]{:S(2)}) copy-start(bf16[1024,256]{1,0:T(8,128)(2,1)} %param.41) | copy-start | bytes 1572868
  7.2 50.3 %copy-start.4 = (bf16[32,32,256]{2,1,0:T(8,128)(2,1)S(1)}, bf16[32,32,256]{2,1,0:T(8,128)(2,1)}, u32[]{:S(2)}) copy-start(bf16[32,32,256]{2,1,0:T(8,128)(2,1)} %param.23) | copy-start | bytes 1572868
  7.2 50.3 %copy-start.23 = (f32[256]{0:T(256)S(1)}, f32[256]{0:T(256)}, u32[]{:S(2)}) copy-start(f32[256]{0:T(256)} %param.33) | copy-start | bytes 3076
  7.2 50.3 %copy-start.17 = (bf16[256,256]{1,0:T(8,128)(2,1)S(1)}, bf16[256,256]{1,0:T(8,128)(2,1)}, u32[]{:S(2)}) copy-start(bf16[256,256]{1,0:T(8,128)(2,1)} %param.34) | copy-start | bytes 393220
  7.2 78.9 %all-gather.3.cloned.1.call-start = ((), (), s32[]{:S(2)}) async-start(), calls=%async_computation.2 | async-start | bytes 4718592 | tf_op jit(solution)/shard_map/all_gather | solution.py:119
  42.5 27.9 %all-to-all-start.1 = ((bf16[4,2,1024]{2,1,0:T(2,128)(2,1)}), bf16[4,2,1024]{2,1,0:T(2,128)(2,1)S(1)}, u32[]{:S(2)}, u32[]{:S(2)}) async-start(bf16[4,2,1024]{2,1,0:T(2,128)(2,1)} %reshape.217), calls=%async_computation.1 | async-start | bytes 32768 | tf_op jit(solution)/shard_map/all_to_all | solution.py:130
  55.1 2.3 %copy-start.11 = (f32[32,32]{1,0:T(8,128)}, f32[32,32]{1,0:T(8,128)S(1)}, u32[]{:S(2)}) copy-start(f32[32,32]{1,0:T(8,128)S(1)} %add_rsqrt_fusion.3) | copy-start | bytes 12292
  70.5 22.2 %copy-start.21 = (bf16[256,32]{0,1:T(8,128)(2,1)S(1)}, bf16[256,32]{0,1:T(8,128)(2,1)}, u32[]{:S(2)}) copy-start(bf16[256,32]{0,1:T(8,128)(2,1)} %param.29) | copy-start | bytes 49156
  70.5 22.2 %copy-start.22 = (f32[256]{0:T(256)S(1)}, f32[256]{0:T(256)}, u32[]{:S(2)}) copy-start(f32[256]{0:T(256)} %param.27) | copy-start | bytes 3076
  86.1 3.5 %copy-start.1 = (bf16[32,256,256]{2,1,0:T(8,128)(2,1)S(1)}, bf16[32,256,256]{2,1,0:T(8,128)(2,1)}, u32[]{:S(2)}) copy-start(bf16[32,256,256]{2,1,0:T(8,128)(2,1)} %all-gather.3.cloned.1.call-done) | copy-start | bytes 12582916
  92.1 0.6 copy-start.9
  102.4 13.8 %all-to-all-start = ((bf16[4,2,32768]{2,1,0:T(2,128)(2,1)}), bf16[4,2,32768]{2,1,0:T(2,128)(2,1)S(1)}, u32[]{:S(2)}, u32[]{:S(2)}) async-start(bf16[4,2,32768]{2,1,0:T(2,128)(2,1)} %reshape.215), calls=%async_computation | async-start | bytes 1048576 | tf_op jit(solution)/shard_map/all_to_all | solution.py:129
  106.1 5.8 %copy-start.2 = (bf16[32,256,256]{2,1,0:T(8,128)(2,1)S(1)}, bf16[32,256,256]{2,1,0:T(8,128)(2,1)}, u32[]{:S(2)}) copy-start(bf16[32,256,256]{2,1,0:T(8,128)(2,1)} %all-gather.3.cloned.1.call-done) | copy-start | bytes 12582916
  106.1 5.8 %copy-start.10 = (f32[32,256]{1,0:T(8,128)S(1)}, f32[32,256]{1,0:T(8,128)}, u32[]{:S(2)}) copy-start(f32[32,256]{1,0:T(8,128)} %copy-done.9) | copy-start | bytes 98308
  106.1 5.8 %copy-start.18 = (bf16[256,256]{1,0:T(8,128)(2,1)S(1)}, bf16[256,256]{1,0:T(8,128)(2,1)}, u32[]{:S(2)}) copy-start(bf16[256,256]{1,0:T(8,128)(2,1)} %param.35) | copy-start | bytes 393220
  106.1 5.8 %copy-start.24 = (f32[256]{0:T(256)S(1)}, f32[256]{0:T(256)}, u32[]{:S(2)}) copy-start(f32[256]{0:T(256)} %param.33) | copy-start | bytes 3076
  117.3 6.0 %copy-start.16 = (bf16[1024,128]{1,0:T(8,128)(2,1)S(1)}, bf16[1024,128]{1,0:T(8,128)(2,1)}, u32[]{:S(2)}) copy-start(bf16[1024,128]{1,0:T(8,128)(2,1)} %param.30) | copy-start | bytes 786436
  117.3 6.0 %copy-start.27 = (s32[2]{0:T(128)S(1)}, s32[2]{0:T(128)}, u32[]{:S(2)}) copy-start(s32[2]{0:T(128)} %iota_multiply_fusion) | copy-start | bytes 28
  123.3 15.9 %copy-start.6 = (f32[32,64,128]{2,1,0:T(8,128)S(1)}, f32[32,64,128]{2,1,0:T(8,128)}, u32[]{:S(2)}) copy-start(f32[32,64,128]{2,1,0:T(8,128)} %param.26) | copy-start | bytes 3145732
  139.2 2.6 %copy-start.13 = (bf16[128,8]{0,1:T(8,128)(2,1)S(1)}, bf16[128,8]{0,1:T(8,128)(2,1)}, u32[]{:S(2)}) copy-start(bf16[128,8]{0,1:T(8,128)(2,1)} %param.32) | copy-start | bytes 6148
  139.2 2.6 %copy-start.14 = (f32[128]{0:T(128)S(1)}, f32[128]{0:T(128)}, u32[]{:S(2)}) copy-start(f32[128]{0:T(128)} %param.31) | copy-start | bytes 1540
  139.2 11.5 %copy-start.8 = (f32[4,8,32,8]{2,3,1,0:T(8,128)S(1)}, f32[4,8,32,8]{2,3,1,0:T(8,128)}, u32[]{:S(2)}) copy-start(f32[4,8,32,8]{2,3,1,0:T(8,128)} %custom-call.2) | copy-start | bytes 98308
  140.9 1.0 copy-start.3
  211.1 6.0 %copy-start.7 = (f32[4,8,32,256]{3,2,1,0:T(8,128)S(1)}, f32[4,8,32,256]{3,2,1,0:T(8,128)}, u32[]{:S(2)}) copy-start(f32[4,8,32,256]{3,2,1,0:T(8,128)} %get-tuple-element.88) | copy-start | bytes 3145732
  213.7 4.6 %copy-start.5 = (bf16[32,32,256]{2,1,0:T(8,128)(2,1)S(1)}, bf16[32,32,256]{2,1,0:T(8,128)(2,1)}, u32[]{:S(2)}) copy-start(bf16[32,32,256]{2,1,0:T(8,128)(2,1)} %param.23) | copy-start | bytes 1572868
  213.7 4.6 %copy-start.12 = (f32[32,32]{1,0:T(8,128)S(1)}, f32[32,32]{1,0:T(8,128)}, u32[]{:S(2)}) copy-start(f32[32,32]{1,0:T(8,128)} %copy-done.11) | copy-start | bytes 12292
  213.7 4.6 %copy-start.19 = (bf16[256,256]{1,0:T(8,128)(2,1)S(1)}, bf16[256,256]{1,0:T(8,128)(2,1)}, u32[]{:S(2)}) copy-start(bf16[256,256]{1,0:T(8,128)(2,1)} %param.38) | copy-start | bytes 393220
  213.7 4.6 %copy-start.20 = (bf16[256,256]{1,0:T(8,128)(2,1)S(1)}, bf16[256,256]{1,0:T(8,128)(2,1)}, u32[]{:S(2)}) copy-start(bf16[256,256]{1,0:T(8,128)(2,1)} %param.37) | copy-start | bytes 393220
  213.7 4.6 %copy-start.25 = (f32[256]{0:T(256)S(1)}, f32[256]{0:T(256)}, u32[]{:S(2)}) copy-start(f32[256]{0:T(256)} %param.33) | copy-start | bytes 3076
  218.3 2.4 %copy-start.15 = (bf16[256,1024]{1,0:T(8,128)(2,1)S(1)}, bf16[256,1024]{1,0:T(8,128)(2,1)}, u32[]{:S(2)}) copy-start(bf16[256,1024]{1,0:T(8,128)(2,1)} %param.40) | copy-start | bytes 1572868
  218.3 2.4 %copy-start.26 = (f32[256]{0:T(256)S(1)}, f32[256]{0:T(256)}, u32[]{:S(2)}) copy-start(f32[256]{0:T(256)} %param.39) | copy-start | bytes 3076
Sparse Core Ops, SparseCore 0:
  10.2 75.8 all-gather.2
